TPU v7x, 32 devices: a whole 2x2x4 slice. The times are simulated.
32 devices in a mesh: gz: 8 (over z, y), gy: 4 (over x, core).
Axes of the slice: x: 2, y: 2, z: 4, core: 2. Of those that a mesh axis runs over, the one named last changes fastest.
Arguments:
- orbitals: bfloat16 [96, 96, 96, 256], P('gz', 'gy'), may hold values from -6 to 6
- pair_list: int32 [64, 2], replicated, may hold values from 0 to 255
- box_anchor: int32 [256, 3], replicated, may hold values from 0 to 95
- pair_live: int32 [64], replicated, may hold values from 0 to 1, as said below
Outputs:
- gradient: float32 [96, 96, 96, 256], P('gz', 'gy')
Inputs may be any that keep to these rules, and one draw needn't show every extreme that they name: `pair_live`: in each owner's block of 2 slots the live slots come first; at least one slot of every block is live, some block has all 2 live, and some other block has exactly one live.
All inputs are finite; a program needn't handle non-finite values.
Results may differ from a plain program's by a relative error of at most 0.0035.
Values may be sent and summed in bfloat16 or wider, within the bound.
A program may use at most 192 MiB of HBM per device.

v0:
```python
import jax
import jax.numpy as jnp
from jax import lax
from jax.sharding import PartitionSpec as P

B = 64


def poisson_box(density):
    side = density.shape[-1]
    index = jnp.arange(1, side + 1).astype(jnp.float32)
    table = jnp.sqrt(2.0 / (side + 1.0)) * jnp.sin(
        jnp.pi * index[:, None] * index[None, :] / (side + 1.0)
    )
    eigen = 2.0 - 2.0 * jnp.cos(jnp.pi * index / (side + 1.0))
    denom = eigen[:, None, None] + eigen[None, :, None] + eigen[None, None, :]
    hp = lax.Precision.HIGHEST

    def apply_all(field):
        field = jnp.einsum("...abc,ai->...ibc", field, table, precision=hp)
        field = jnp.einsum("...ibc,bj->...ijc", field, table, precision=hp)
        return jnp.einsum("...ijc,ck->...ijk", field, table, precision=hp)

    return apply_all(apply_all(density) / denom)


def body(orbitals, pair_list, box_anchor, pair_live):
    depth, rows, across, norb = orbitals.shape
    n_gz = lax.axis_size("gz")
    n_gy = lax.axis_size("gy")
    owners = n_gz * n_gy
    pairs = pair_list.shape[0]
    per_dev = pairs // owners
    slots = 2 * per_dev
    side = B
    extent = depth * n_gz
    firsts = pair_list[:, 0]
    chosen = jnp.take(orbitals, pair_list.reshape(-1), axis=3)
    width = chosen.shape[2]
    outgoing = chosen.reshape(depth, rows, width, n_gz, n_gy, slots)
    flat_send = outgoing.reshape(depth, rows, width, owners, slots)
    incoming = lax.all_to_all(
        flat_send, ("gz", "gy"), split_axis=3, concat_axis=3, tiled=True
    ).reshape(depth, rows, width, n_gz, n_gy, slots)
    grids = jnp.transpose(incoming, (5, 3, 0, 4, 1, 2)).reshape(per_dev, 2, extent, extent, width)
    owner = lax.axis_index(("gz", "gy"))
    mine = lax.dynamic_slice_in_dim(pair_list, owner * per_dev, per_dev, 0)
    live = lax.dynamic_slice_in_dim(pair_live, owner * per_dev, per_dev, 0)
    anchors = box_anchor[mine[:, 0]]

    def cut_box(grid, anchor):
        grid = jnp.roll(grid, -anchor[0], axis=0)
        grid = jnp.roll(grid, -anchor[1], axis=1)
        grid = jnp.roll(grid, -anchor[2], axis=2)
        return grid[:side, :side, :side]

    def both_boxes(pair_grids, anchor):
        return jax.vmap(cut_box, in_axes=(0, None))(pair_grids, anchor)

    boxes = jax.vmap(both_boxes)(grids, anchors)
    left = boxes[:, 0].astype(jnp.float32)
    right = boxes[:, 1].astype(jnp.float32)
    potential = poisson_box(left * right)
    weight = live.astype(jnp.float32)[:, None, None, None]
    term = (potential * right * weight).astype(jnp.bfloat16)

    def place_box(box, anchor):
        pad_x = across - side
        grid = jnp.pad(box, ((0, extent - side), (0, extent - side), (0, pad_x)))
        grid = jnp.roll(grid, anchor[0], axis=0)
        grid = jnp.roll(grid, anchor[1], axis=1)
        grid = jnp.roll(grid, anchor[2], axis=2)
        return grid

    placed = jax.vmap(place_box)(term, anchors)
    back_send = jnp.transpose(
        placed.reshape(per_dev, n_gz, depth, n_gy, rows, width), (2, 4, 5, 1, 3, 0)
    )
    flat_back = back_send.reshape(depth, rows, width, owners, per_dev)
    back = lax.all_to_all(flat_back, ("gz", "gy"), split_axis=3, concat_axis=3, tiled=True)
    contrib = back.reshape(depth, rows, width, pairs)
    selector = (firsts[:, None] == jnp.arange(norb)[None, :]).astype(jnp.bfloat16)
    action = jnp.dot(contrib.reshape(-1, pairs), selector, preferred_element_type=jnp.float32)
    action_low = action.astype(jnp.bfloat16)
    flat = orbitals.reshape(-1, norb)
    partial_tiles = lax.dot_general(
        flat, action_low, (((0,), (0,)), ((), ())), preferred_element_type=jnp.float32
    )
    summed = lax.psum(partial_tiles, ("gz", "gy"))
    tiles = (summed / (float(B) ** 3 / 4.0)).astype(jnp.bfloat16)
    gradient = action - jnp.dot(flat, tiles, preferred_element_type=jnp.float32)
    return gradient.reshape(depth, rows, across, norb)


def solution(mesh):
    return jax.shard_map(
        body,
        mesh=mesh,
        in_specs=(P("gz", "gy", None, None), P(), P(), P()),
        out_specs=P("gz", "gy", None, None),
        check_vma=False,
    )
```

profile of v0, /device:TPU:0, one launch (start us, length us, event | category | flops | bytes accessed | tf_op | source)
XLA Modules:
  0.0 842.0 jit_solution(8082996493727971002)
XLA Ops:
  7.5 22.4 %copy.44 = bf16[12,24,96,256]{2,1,0,3:T(8,128)(2,1)} copy(bf16[12,24,96,256]{3,2,1,0:T(8,128)(2,1)} %param.4) | data formatting | bytes 28311552 | tf_op args[0]
  29.9 13.6 %gather_fusion = bf16[128,12,24,96]{3,2,1,0:T(8,128)(2,1)} fusion(bf16[12,24,96,256]{2,1,0,3:T(8,128)(2,1)} %copy.44, s32[1024]{0:T(1024)S(1)} %pad_clamp_fusion.1), kind=kCustom, calls=%fused_computation | custom fusion | bytes 14156288 | tf_op jit(solution)/shard_map/jit(_take)/gather | solution.py:38
  43.5 9.6 %copy.45 = bf16[12,24,96,128]{2,1,3,0:T(8,128)(2,1)} copy(bf16[12,24,96,128]{2,1,0,3:T(8,128)(2,1)} %bitcast.113) | data formatting | bytes 14155776 | tf_op jit(solution)/shard_map/jit(_take)/gather | solution.py:38
  53.2 8.6 %broadcast_select_fusion = bf16[12,24,96,32,4]{2,1,4,3,0:T(8,128)(2,1)} fusion(bf16[12,24,96,32,4]{2,1,4,3,0:T(8,128)(2,1)} %bitcast.112, pred[32,4]{1,0:T(8,128)(4,1)S(1)} %compare_and_fusion), kind=kLoop, calls=%fused_computation.24 | loop fusion | flops 3538944 | bytes 14155904 | tf_op jit(solution)/shard_map/jit(_take)/select_n | solution.py:38
  61.7 10.2 %copy.46 = bf16[12,24,96,32,4]{2,1,4,0,3:T(8,128)(2,1)} copy(bf16[12,24,96,32,4]{2,1,4,3,0:T(8,128)(2,1)} %broadcast_select_fusion) | data formatting | bytes 14155776 | tf_op jit(solution)/shard_map/jit(_take)/select_n | solution.py:38
  71.9 7.9 all-to-all-start
  81.8 206.9 %all-to-all-done = bf16[12,24,96,32,4]{2,1,4,0,3:T(8,128)(2,1)} async-done(((bf16[12,24,96,32,4]{2,1,4,0,3:T(8,128)(2,1)}), bf16[12,24,96,32,4]{2,1,4,0,3:T(8,128)(2,1)}, u32[]{:S(2)}, u32[]{:S(2)}) %all-to-all-start) | async-done | bytes 7077920 | tf_op jit(solution)/shard_map/all_to_all | solution.py:42
  288.7 10.2 %copy.48 = bf16[4,8,12,4,24,96]{5,4,3,2,1,0:T(8,128)(2,1)} copy(bf16[4,8,12,4,24,96]{5,4,0,2,3,1:T(8,128)(2,1)} %bitcast.9) | data formatting | bytes 14155776 | tf_op jit(solution)/shard_map/transpose | solution.py:45
  298.9 16.0 %pad_maximum_fusion = bf16[2,2,192,96,96]{4,3,2,1,0:T(8,128)(2,1)} fusion(bf16[2,2,96,96,96]{4,3,2,1,0:T(8,128)(2,1)} %bitcast.111), kind=kLoop, calls=%fused_computation.16 | loop fusion | flops 7077888 | bytes 21233664 | tf_op jit(solution)/shard_map/vmap(vmap(jit(_roll_dynamic)))/concatenate | solution.py:52
  320.1 14.5 %while.6 = (s32[]{:T(128)}, bf16[2,2,192,96,96]{4,3,2,1,0:T(8,128)(2,1)}, s32[2,4]{1,0:T(2,128)S(1)}, bf16[2,2,96,96,96]{4,3,2,1,0:T(8,128)(2,1)}, s32[]{:T(128)}) while((s32[]{:T(128)}, bf16[2,2,192,96,96]{4,3,2,1,0:T(8,128)(2,1)}, s32[2,4]{1,0:T(2,128)S(1)}, bf16[2,2,96,96,96]{4,3,2,1,0:T(8,128)(2,1)}, s32[]{:T(128)}) %tuple.99), condition=%wide.while_cond, body=%wide.while_body.sunk | while | flops 2 | bytes 9438833 | solution.py:52
  320.7 6.7 dynamic-slice_dynamic-update-slice_fusion.10
  334.6 18.2 %pad_maximum_fusion.1 = bf16[2,2,96,192,96]{4,3,2,1,0:T(8,128)(2,1)} fusion(bf16[2,2,96,96,96]{4,3,2,1,0:T(8,128)(2,1)} %get-tuple-element.12), kind=kLoop, calls=%fused_computation.17 | loop fusion | flops 28311552 | bytes 21233664 | tf_op jit(solution)/shard_map/vmap(vmap(jit(_roll_dynamic)))/concatenate | solution.py:53
  357.9 18.6 %while.7 = (s32[]{:T(128)}, bf16[2,2,96,192,96]{4,3,2,1,0:T(8,128)(2,1)}, s32[2,4]{1,0:T(2,128)S(1)}, bf16[2,2,96,96,96]{4,3,2,1,0:T(8,128)(2,1)}, s32[]{:T(128)}) while((s32[]{:T(128)}, bf16[2,2,96,192,96]{4,3,2,1,0:T(8,128)(2,1)}, s32[2,4]{1,0:T(2,128)S(1)}, bf16[2,2,96,96,96]{4,3,2,1,0:T(8,128)(2,1)}, s32[]{:T(128)}) %tuple.102), condition=%wide.while_cond.1, body=%wide.while_body.1.sunk | while | flops 2 | bytes 9438833 | solution.py:53
  358.6 8.7 %dynamic-slice_dynamic-update-slice_fusion.11 = bf16[2,2,96,96,96]{4,3,2,1,0:T(8,128)(2,1)} fusion(bf16[2,2,96,96,96]{4,3,2,1,0:T(8,128)(2,1)} %get-tuple-element.323, s32[]{:T(128)} %get-tuple-element.320, bf16[2,2,96,192,96]{4,3,2,1,0:T(8,128)(2,1)} %get-tuple-element.326, s32[]{:T(128)} %bitcast.98, s32[]{:T(128)} %bitcast.99), kind=kLoop, calls=%fused_computation.4.clone.1 | loop fusion | bytes 9438720 | tf_op jit(solution)/shard_map/vmap(vmap(jit(_roll_dynamic)))/gather
  368.0 8.6 %dynamic-slice_dynamic-update-slice_fusion.11 = bf16[2,2,96,96,96]{4,3,2,1,0:T(8,128)(2,1)} fusion(bf16[2,2,96,96,96]{4,3,2,1,0:T(8,128)(2,1)} %get-tuple-element.323, s32[]{:T(128)} %get-tuple-element.320, bf16[2,2,96,192,96]{4,3,2,1,0:T(8,128)(2,1)} %get-tuple-element.326, s32[]{:T(128)} %bitcast.98, s32[]{:T(128)} %bitcast.99), kind=kLoop, calls=%fused_computation.4.clone.1 | loop fusion | bytes 9438720 | tf_op jit(solution)/shard_map/vmap(vmap(jit(_roll_dynamic)))/gather
  376.5 20.0 %pad_maximum_fusion.2 = bf16[2,2,96,96,192]{4,3,2,1,0:T(8,128)(2,1)} fusion(bf16[2,2,96,96,96]{4,3,2,1,0:T(8,128)(2,1)} %get-tuple-element.20), kind=kLoop, calls=%fused_computation.18 | loop fusion | flops 28311552 | bytes 21233664 | tf_op jit(solution)/shard_map/vmap(vmap(jit(_roll_dynamic)))/concatenate | solution.py:54
  396.6 18.8 %while.8 = (s32[]{:T(128)}, bf16[2,2,96,96,192]{4,3,2,1,0:T(8,128)(2,1)}, s32[2,4]{1,0:T(2,128)S(1)}, bf16[2,2,96,96,96]{4,3,2,0,1:T(8,128)(2,1)}, s32[]{:T(128)}) while((s32[]{:T(128)}, bf16[2,2,96,96,192]{4,3,2,1,0:T(8,128)(2,1)}, s32[2,4]{1,0:T(2,128)S(1)}, bf16[2,2,96,96,96]{4,3,2,0,1:T(8,128)(2,1)}, s32[]{:T(128)}) %tuple.105), condition=%wide.while_cond.2, body=%wide.while_body.2.sunk | while | flops 2 | bytes 9438833 | solution.py:54
  397.2 8.7 %bitcast_dynamic-update-slice_fusion.2 = bf16[2,2,96,96,96]{4,3,2,0,1:T(8,128)(2,1)} fusion(bf16[2,2,96,96,96]{4,3,2,0,1:T(8,128)(2,1)} %get-tuple-element.338, s32[]{:T(128)} %get-tuple-element.335, bf16[2,2,96,96,192]{4,3,2,1,0:T(8,128)(2,1)} %get-tuple-element.341, s32[]{:T(128)} %bitcast.101, s32[]{:T(128)} %bitcast.102), kind=kLoop, calls=%fused_computation.6.clone.1 | loop fusion | bytes 9438720 | tf_op jit(solution)/shard_map/vmap(vmap(jit(_roll_dynamic)))/gather
  406.5 8.8 %bitcast_dynamic-update-slice_fusion.2 = bf16[2,2,96,96,96]{4,3,2,0,1:T(8,128)(2,1)} fusion(bf16[2,2,96,96,96]{4,3,2,0,1:T(8,128)(2,1)} %get-tuple-element.338, s32[]{:T(128)} %get-tuple-element.335, bf16[2,2,96,96,192]{4,3,2,1,0:T(8,128)(2,1)} %get-tuple-element.341, s32[]{:T(128)} %bitcast.101, s32[]{:T(128)} %bitcast.102), kind=kLoop, calls=%fused_computation.6.clone.1 | loop fusion | bytes 9438720 | tf_op jit(solution)/shard_map/vmap(vmap(jit(_roll_dynamic)))/gather
  425.0 6.6 fusion.13
  441.9 6.8 fusion.9
  462.1 10.2 %while.9 = (s32[]{:T(128)}, bf16[2,192,96,96]{3,2,1,0:T(8,128)(2,1)}, s32[2,4]{1,0:T(2,128)S(1)}, bf16[2,96,96,96]{3,2,1,0:T(8,128)(2,1)}, s32[]{:T(128)}) while((s32[]{:T(128)}, bf16[2,192,96,96]{3,2,1,0:T(8,128)(2,1)}, s32[2,4]{1,0:T(2,128)S(1)}, bf16[2,96,96,96]{3,2,1,0:T(8,128)(2,1)}, s32[]{:T(128)}) %tuple.108), condition=%wide.while_cond.3, body=%wide.while_body.3.sunk | while | flops 2 | bytes 4720241 | solution.py:70
  472.2 10.1 %pad_maximum_fusion.4 = bf16[2,96,192,96]{3,2,1,0:T(8,128)(2,1)} fusion(bf16[2,96,96,96]{3,2,1,0:T(8,128)(2,1)} %get-tuple-element.36), kind=kLoop, calls=%fused_computation.22 | loop fusion | flops 14155776 | bytes 10616832 | tf_op jit(solution)/shard_map/vmap(jit(_roll_dynamic))/concatenate | solution.py:71
  485.0 12.3 %while.10 = (s32[]{:T(128)}, bf16[2,96,192,96]{3,2,1,0:T(8,128)(2,1)}, s32[2,4]{1,0:T(2,128)S(1)}, bf16[2,96,96,96]{3,2,1,0:T(8,128)(2,1)}, s32[]{:T(128)}) while((s32[]{:T(128)}, bf16[2,96,192,96]{3,2,1,0:T(8,128)(2,1)}, s32[2,4]{1,0:T(2,128)S(1)}, bf16[2,96,96,96]{3,2,1,0:T(8,128)(2,1)}, s32[]{:T(128)}) %tuple.111), condition=%wide.while_cond.4, body=%wide.while_body.4.sunk | while | flops 2 | bytes 4720241 | solution.py:71
  497.4 11.6 %pad_maximum_fusion.5 = bf16[2,96,96,192]{3,2,1,0:T(8,128)(2,1)} fusion(bf16[2,96,96,96]{3,2,1,0:T(8,128)(2,1)} %get-tuple-element.44), kind=kLoop, calls=%fused_computation.23 | loop fusion | flops 14155776 | bytes 10616832 | tf_op jit(solution)/shard_map/vmap(jit(_roll_dynamic))/concatenate | solution.py:72
  511.7 12.9 %while.11 = (s32[]{:T(128)}, bf16[2,96,96,192]{3,2,1,0:T(8,128)(2,1)}, s32[2,4]{1,0:T(2,128)S(1)}, bf16[2,96,96,96]{3,2,1,0:T(8,128)(2,1)}, s32[]{:T(128)}) while((s32[]{:T(128)}, bf16[2,96,96,192]{3,2,1,0:T(8,128)(2,1)}, s32[2,4]{1,0:T(2,128)S(1)}, bf16[2,96,96,96]{3,2,1,0:T(8,128)(2,1)}, s32[]{:T(128)}) %tuple.114), condition=%wide.while_cond.5, body=%wide.while_body.5.sunk | while | flops 2 | bytes 4720241 | solution.py:72
  535.5 105.1 %all-to-all-done.1 = bf16[12,24,96,32,2]{2,1,4,0,3:T(8,128)(2,1)} async-done(((bf16[12,24,96,32,2]{2,1,4,0,3:T(8,128)(2,1)}), bf16[12,24,96,32,2]{2,1,4,0,3:T(8,128)(2,1)}, u32[]{:S(2)}, u32[]{:S(2)}) %all-to-all-start.1) | async-done | bytes 3538976 | tf_op jit(solution)/shard_map/all_to_all | solution.py:80
  646.0 8.1 reshape_reshape.4
  654.1 12.0 %fusion.32 = f32[27648,256]{1,0:T(8,128)} fusion(bf16[27648,64]{0,1:T(8,128)(2,1)S(1)} %reshape_reshape.4, s32[64]{0:T(128)S(1)} %slice_bitcast_fusion), kind=kOutput, calls=%fused_computation.49 | convolution fusion | flops 905986048 | bytes 31850752 | tf_op jit(solution)/shard_map/dot_general | solution.py:83
  666.1 17.6 %fusion.28 = f32[256,256]{0,1:T(8,128)} fusion(bf16[27648,256]{1,0:T(8,128)(2,1)} %bitcast.109, f32[27648,256]{1,0:T(8,128)} %fusion.32), kind=kOutput, calls=%fused_computation.44 | convolution fusion | flops 3630956544 | bytes 42729472 | tf_op jit(solution)/shard_map/dot_general | solution.py:86
  683.8 126.0 %all-reduce.7.cloned.1.call-done = f32[256,256]{0,1:T(8,128)} async-done(((f32[256,256]{0,1:T(8,128)}), f32[256,256]{0,1:T(8,128)}) %all-reduce.7.cloned.1.call-update) | async-done | bytes 262160 | tf_op jit(solution)/shard_map/psum | solution.py:89
  809.7 25.2 %fusion = f32[27648,256]{1,0:T(8,128)} fusion(f32[27648,256]{1,0:T(8,128)} %fusion.32, bf16[27648,256]{1,0:T(8,128)(2,1)} %bitcast.110, f32[256,256]{0,1:T(8,128)} %all-reduce.7.cloned.1.call-done), kind=kOutput, calls=%fused_computation.15 | convolution fusion | flops 3631087616 | bytes 71041024 | tf_op jit(solution)/shard_map/dot_general | solution.py:91
  (79 shorter events, 113.6 us)
Async XLA Ops:
  71.9 7.9 copy-start
  71.9 8.9 %copy-start.2 = (s32[64]{0:T(128)S(1)}, s32[64]{0:T(128)}, u32[]{:S(2)}) copy-start(s32[64]{0:T(128)} %param.7) | copy-start | bytes 772
  71.9 216.8 %all-to-all-start = ((bf16[12,24,96,32,4]{2,1,4,0,3:T(8,128)(2,1)}), bf16[12,24,96,32,4]{2,1,4,0,3:T(8,128)(2,1)}, u32[]{:S(2)}, u32[]{:S(2)}) async-start(bf16[12,24,96,32,4]{2,1,4,0,3:T(8,128)(2,1)} %copy.46), calls=%async_computation | async-start | bytes 18874368 | tf_op jit(solution)/shard_map/all_to_all | solution.py:42
  528.3 7.2 copy-start.1
  531.9 108.8 %all-to-all-start.1 = ((bf16[12,24,96,32,2]{2,1,4,0,3:T(8,128)(2,1)}), bf16[12,24,96,32,2]{2,1,4,0,3:T(8,128)(2,1)}, u32[]{:S(2)}, u32[]{:S(2)}) async-start(bf16[12,24,96,32,2]{2,1,4,0,3:T(8,128)(2,1)} %copy.62), calls=%async_computation.1 | async-start | bytes 9437184 | tf_op jit(solution)/shard_map/all_to_all | solution.py:80
  535.5 274.3 %all-reduce.7.cloned.1.call-start = ((), (), s32[]{:S(2)}) async-start(), calls=%async_computation.2 | async-start | bytes 524288 | tf_op jit(solution)/shard_map/psum | solution.py:89
Sparse Core Ops, SparseCore 0:
  683.9 125.7 all-reduce.6
where the time goes:
time: 849 us; the launch traced here: 842 us
  waiting for transfers between devices  438 us (52%)
  local copies, waits for them, and re-layouts  195 us (23%)
  other arithmetic  93.4 us (11%)
  matrix products  90.2 us (11%)
  between operations  13.9 us (2%)
  starting transfers between devices  11.5 us (1%)
    all_to_all x1, waiting for transfers between devices, body(): lax.all_to_all(flat_send, ('gz', 'gy'), split_axis=3, concat_axis=3, tile...  207 us
    psum x1, waiting for transfers between devices, body(): summed = lax.psum(partial_tiles, ('gz', 'gy'))  126 us
    all_to_all x1, waiting for transfers between devices, body(): lax.all_to_all(flat_back, ('gz', 'gy'), split_axis=3, concat_axis=3, tile...  105 us
    gather x36, local copies, waits for them, and re-layouts  87.1 us
    unnamed x15, local copies, waits for them, and re-layouts  41.7 us
    dot_general x1, matrix products, body(): gradient = action - jnp.dot(flat, tiles, preferred_element_type=jnp.float32)  25.2 us
    gather x2, local copies, waits for them, and re-layouts, body(): chosen = jnp.take(orbitals, pair_list.reshape(-1), axis=3)  23.2 us
    concatenate x1, other arithmetic, cut_box(): grid = jnp.roll(grid, -anchor[2], axis=2)  20 us
  transfers between devices with their start and end apart: 3, of which 3 were waited for; matrix products, arithmetic and copies ran while one was open for 0% of the time, Pallas kernels for 0%

commit v1 on v0

--- a/solution.py
+++ b/solution.py
@@ -86,7 +86,8 @@
     partial_tiles = lax.dot_general(
         flat, action_low, (((0,), (0,)), ((), ())), preferred_element_type=jnp.float32
     )
-    summed = lax.psum(partial_tiles, ("gz", "gy"))
+    one_axis = lax.psum(partial_tiles, "gy")
+    summed = lax.psum(one_axis, "gz")
     tiles = (summed / (float(B) ** 3 / 4.0)).astype(jnp.bfloat16)
     gradient = action - jnp.dot(flat, tiles, preferred_element_type=jnp.float32)
     return gradient.reshape(depth, rows, across, norb)

time: 849 us -> 830 us (0.978)
  waiting for transfers between devices: 438 us -> 418 us
    psum x1 -> x2, waiting for transfers between devices: 126 us -> 106 us  [the longest x1 74.4 us: body(): summed = lax.psum(one_axis, 'gz')]
  transfers between devices with their start and end apart: 3 -> 4, of which waited for: 3 -> 4; matrix products, arithmetic and copies ran while one was open for 0% -> 0% of each run, Pallas kernels for 0% -> 0%
where the time goes in v1:
time: 830 us; the launch traced here: 822 us
  waiting for transfers between devices  418 us (50%)
  local copies, waits for them, and re-layouts  195 us (23%)
  other arithmetic  93.4 us (11%)
  matrix products  90.3 us (11%)
  between operations  13.9 us (2%)
  starting transfers between devices  11.6 us (1%)
    all_to_all x1, waiting for transfers between devices, body(): lax.all_to_all(flat_send, ('gz', 'gy'), split_axis=3, concat_axis=3, tile...  207 us
    all_to_all x1, waiting for transfers between devices, body(): lax.all_to_all(flat_back, ('gz', 'gy'), split_axis=3, concat_axis=3, tile...  105 us
    gather x36, local copies, waits for them, and re-layouts  87.1 us
    psum x1, waiting for transfers between devices, body(): summed = lax.psum(one_axis, 'gz')  74.4 us
    unnamed x15, local copies, waits for them, and re-layouts  41.7 us
    psum x1, waiting for transfers between devices, body(): one_axis = lax.psum(partial_tiles, 'gy')  31.6 us
    dot_general x1, matrix products, body(): gradient = action - jnp.dot(flat, tiles, preferred_element_type=jnp.float32)  25.2 us
    gather x2, local copies, waits for them, and re-layouts, body(): chosen = jnp.take(orbitals, pair_list.reshape(-1), axis=3)  23.2 us
  transfers between devices with their start and end apart: 4, of which 4 were waited for; matrix products, arithmetic and copies ran while one was open for 0% of the time, Pallas kernels for 0%

profile of v1, /device:TPU:0, one launch (start us, length us, event | category | flops | bytes accessed | tf_op | source)
XLA Modules:
  0.0 822.1 jit_solution(18044069387482050391)
XLA Ops:
  7.5 22.4 %copy.44 = bf16[12,24,96,256]{2,1,0,3:T(8,128)(2,1)} copy(bf16[12,24,96,256]{3,2,1,0:T(8,128)(2,1)} %param.4) | data formatting | bytes 28311552 | tf_op args[0]
  29.9 13.6 %gather_fusion = bf16[128,12,24,96]{3,2,1,0:T(8,128)(2,1)} fusion(bf16[12,24,96,256]{2,1,0,3:T(8,128)(2,1)} %copy.44, s32[1024]{0:T(1024)S(1)} %pad_clamp_fusion.1), kind=kCustom, calls=%fused_computation | custom fusion | bytes 14156288 | tf_op jit(solution)/shard_map/jit(_take)/gather | solution.py:38
  43.5 9.6 %copy.45 = bf16[12,24,96,128]{2,1,3,0:T(8,128)(2,1)} copy(bf16[12,24,96,128]{2,1,0,3:T(8,128)(2,1)} %bitcast.113) | data formatting | bytes 14155776 | tf_op jit(solution)/shard_map/jit(_take)/gather | solution.py:38
  53.2 8.6 %broadcast_select_fusion = bf16[12,24,96,32,4]{2,1,4,3,0:T(8,128)(2,1)} fusion(bf16[12,24,96,32,4]{2,1,4,3,0:T(8,128)(2,1)} %bitcast.112, pred[32,4]{1,0:T(8,128)(4,1)S(1)} %compare_and_fusion), kind=kLoop, calls=%fused_computation.24 | loop fusion | flops 3538944 | bytes 14155904 | tf_op jit(solution)/shard_map/jit(_take)/select_n | solution.py:38
  61.7 10.2 %copy.46 = bf16[12,24,96,32,4]{2,1,4,0,3:T(8,128)(2,1)} copy(bf16[12,24,96,32,4]{2,1,4,3,0:T(8,128)(2,1)} %broadcast_select_fusion) | data formatting | bytes 14155776 | tf_op jit(solution)/shard_map/jit(_take)/select_n | solution.py:38
  71.9 7.9 all-to-all-start
  81.8 206.9 %all-to-all-done = bf16[12,24,96,32,4]{2,1,4,0,3:T(8,128)(2,1)} async-done(((bf16[12,24,96,32,4]{2,1,4,0,3:T(8,128)(2,1)}), bf16[12,24,96,32,4]{2,1,4,0,3:T(8,128)(2,1)}, u32[]{:S(2)}, u32[]{:S(2)}) %all-to-all-start) | async-done | bytes 7077920 | tf_op jit(solution)/shard_map/all_to_all | solution.py:42
  288.7 10.2 %copy.48 = bf16[4,8,12,4,24,96]{5,4,3,2,1,0:T(8,128)(2,1)} copy(bf16[4,8,12,4,24,96]{5,4,0,2,3,1:T(8,128)(2,1)} %bitcast.9) | data formatting | bytes 14155776 | tf_op jit(solution)/shard_map/transpose | solution.py:45
  298.9 16.0 %pad_maximum_fusion = bf16[2,2,192,96,96]{4,3,2,1,0:T(8,128)(2,1)} fusion(bf16[2,2,96,96,96]{4,3,2,1,0:T(8,128)(2,1)} %bitcast.111), kind=kLoop, calls=%fused_computation.16 | loop fusion | flops 7077888 | bytes 21233664 | tf_op jit(solution)/shard_map/vmap(vmap(jit(_roll_dynamic)))/concatenate | solution.py:52
  320.1 14.5 %while.6 = (s32[]{:T(128)}, bf16[2,2,192,96,96]{4,3,2,1,0:T(8,128)(2,1)}, s32[2,4]{1,0:T(2,128)S(1)}, bf16[2,2,96,96,96]{4,3,2,1,0:T(8,128)(2,1)}, s32[]{:T(128)}) while((s32[]{:T(128)}, bf16[2,2,192,96,96]{4,3,2,1,0:T(8,128)(2,1)}, s32[2,4]{1,0:T(2,128)S(1)}, bf16[2,2,96,96,96]{4,3,2,1,0:T(8,128)(2,1)}, s32[]{:T(128)}) %tuple.99), condition=%wide.while_cond, body=%wide.while_body.sunk | while | flops 2 | bytes 9438833 | solution.py:52
  320.7 6.7 dynamic-slice_dynamic-update-slice_fusion.10
  334.6 18.2 %pad_maximum_fusion.1 = bf16[2,2,96,192,96]{4,3,2,1,0:T(8,128)(2,1)} fusion(bf16[2,2,96,96,96]{4,3,2,1,0:T(8,128)(2,1)} %get-tuple-element.12), kind=kLoop, calls=%fused_computation.17 | loop fusion | flops 28311552 | bytes 21233664 | tf_op jit(solution)/shard_map/vmap(vmap(jit(_roll_dynamic)))/concatenate | solution.py:53
  357.9 18.6 %while.7 = (s32[]{:T(128)}, bf16[2,2,96,192,96]{4,3,2,1,0:T(8,128)(2,1)}, s32[2,4]{1,0:T(2,128)S(1)}, bf16[2,2,96,96,96]{4,3,2,1,0:T(8,128)(2,1)}, s32[]{:T(128)}) while((s32[]{:T(128)}, bf16[2,2,96,192,96]{4,3,2,1,0:T(8,128)(2,1)}, s32[2,4]{1,0:T(2,128)S(1)}, bf16[2,2,96,96,96]{4,3,2,1,0:T(8,128)(2,1)}, s32[]{:T(128)}) %tuple.102), condition=%wide.while_cond.1, body=%wide.while_body.1.sunk | while | flops 2 | bytes 9438833 | solution.py:53
  358.6 8.7 %dynamic-slice_dynamic-update-slice_fusion.11 = bf16[2,2,96,96,96]{4,3,2,1,0:T(8,128)(2,1)} fusion(bf16[2,2,96,96,96]{4,3,2,1,0:T(8,128)(2,1)} %get-tuple-element.323, s32[]{:T(128)} %get-tuple-element.320, bf16[2,2,96,192,96]{4,3,2,1,0:T(8,128)(2,1)} %get-tuple-element.326, s32[]{:T(128)} %bitcast.98, s32[]{:T(128)} %bitcast.99), kind=kLoop, calls=%fused_computation.4.clone.1 | loop fusion | bytes 9438720 | tf_op jit(solution)/shard_map/vmap(vmap(jit(_roll_dynamic)))/gather
  368.0 8.6 %dynamic-slice_dynamic-update-slice_fusion.11 = bf16[2,2,96,96,96]{4,3,2,1,0:T(8,128)(2,1)} fusion(bf16[2,2,96,96,96]{4,3,2,1,0:T(8,128)(2,1)} %get-tuple-element.323, s32[]{:T(128)} %get-tuple-element.320, bf16[2,2,96,192,96]{4,3,2,1,0:T(8,128)(2,1)} %get-tuple-element.326, s32[]{:T(128)} %bitcast.98, s32[]{:T(128)} %bitcast.99), kind=kLoop, calls=%fused_computation.4.clone.1 | loop fusion | bytes 9438720 | tf_op jit(solution)/shard_map/vmap(vmap(jit(_roll_dynamic)))/gather
  376.5 20.0 %pad_maximum_fusion.2 = bf16[2,2,96,96,192]{4,3,2,1,0:T(8,128)(2,1)} fusion(bf16[2,2,96,96,96]{4,3,2,1,0:T(8,128)(2,1)} %get-tuple-element.20), kind=kLoop, calls=%fused_computation.18 | loop fusion | flops 28311552 | bytes 21233664 | tf_op jit(solution)/shard_map/vmap(vmap(jit(_roll_dynamic)))/concatenate | solution.py:54
  396.6 18.8 %while.8 = (s32[]{:T(128)}, bf16[2,2,96,96,192]{4,3,2,1,0:T(8,128)(2,1)}, s32[2,4]{1,0:T(2,128)S(1)}, bf16[2,2,96,96,96]{4,3,2,0,1:T(8,128)(2,1)}, s32[]{:T(128)}) while((s32[]{:T(128)}, bf16[2,2,96,96,192]{4,3,2,1,0:T(8,128)(2,1)}, s32[2,4]{1,0:T(2,128)S(1)}, bf16[2,2,96,96,96]{4,3,2,0,1:T(8,128)(2,1)}, s32[]{:T(128)}) %tuple.105), condition=%wide.while_cond.2, body=%wide.while_body.2.sunk | while | flops 2 | bytes 9438833 | solution.py:54
  397.2 8.7 %bitcast_dynamic-update-slice_fusion.2 = bf16[2,2,96,96,96]{4,3,2,0,1:T(8,128)(2,1)} fusion(bf16[2,2,96,96,96]{4,3,2,0,1:T(8,128)(2,1)} %get-tuple-element.338, s32[]{:T(128)} %get-tuple-element.335, bf16[2,2,96,96,192]{4,3,2,1,0:T(8,128)(2,1)} %get-tuple-element.341, s32[]{:T(128)} %bitcast.101, s32[]{:T(128)} %bitcast.102), kind=kLoop, calls=%fused_computation.6.clone.1 | loop fusion | bytes 9438720 | tf_op jit(solution)/shard_map/vmap(vmap(jit(_roll_dynamic)))/gather
  406.5 8.8 %bitcast_dynamic-update-slice_fusion.2 = bf16[2,2,96,96,96]{4,3,2,0,1:T(8,128)(2,1)} fusion(bf16[2,2,96,96,96]{4,3,2,0,1:T(8,128)(2,1)} %get-tuple-element.338, s32[]{:T(128)} %get-tuple-element.335, bf16[2,2,96,96,192]{4,3,2,1,0:T(8,128)(2,1)} %get-tuple-element.341, s32[]{:T(128)} %bitcast.101, s32[]{:T(128)} %bitcast.102), kind=kLoop, calls=%fused_computation.6.clone.1 | loop fusion | bytes 9438720 | tf_op jit(solution)/shard_map/vmap(vmap(jit(_roll_dynamic)))/gather
  441.9 6.8 fusion.9
  462.1 10.2 %while.9 = (s32[]{:T(128)}, bf16[2,192,96,96]{3,2,1,0:T(8,128)(2,1)}, s32[2,4]{1,0:T(2,128)S(1)}, bf16[2,96,96,96]{3,2,1,0:T(8,128)(2,1)}, s32[]{:T(128)}) while((s32[]{:T(128)}, bf16[2,192,96,96]{3,2,1,0:T(8,128)(2,1)}, s32[2,4]{1,0:T(2,128)S(1)}, bf16[2,96,96,96]{3,2,1,0:T(8,128)(2,1)}, s32[]{:T(128)}) %tuple.108), condition=%wide.while_cond.3, body=%wide.while_body.3.sunk | while | flops 2 | bytes 4720241 | solution.py:70
  472.2 10.1 %pad_maximum_fusion.4 = bf16[2,96,192,96]{3,2,1,0:T(8,128)(2,1)} fusion(bf16[2,96,96,96]{3,2,1,0:T(8,128)(2,1)} %get-tuple-element.36), kind=kLoop, calls=%fused_computation.22 | loop fusion | flops 14155776 | bytes 10616832 | tf_op jit(solution)/shard_map/vmap(jit(_roll_dynamic))/concatenate | solution.py:71
  485.0 12.3 %while.10 = (s32[]{:T(128)}, bf16[2,96,192,96]{3,2,1,0:T(8,128)(2,1)}, s32[2,4]{1,0:T(2,128)S(1)}, bf16[2,96,96,96]{3,2,1,0:T(8,128)(2,1)}, s32[]{:T(128)}) while((s32[]{:T(128)}, bf16[2,96,192,96]{3,2,1,0:T(8,128)(2,1)}, s32[2,4]{1,0:T(2,128)S(1)}, bf16[2,96,96,96]{3,2,1,0:T(8,128)(2,1)}, s32[]{:T(128)}) %tuple.111), condition=%wide.while_cond.4, body=%wide.while_body.4.sunk | while | flops 2 | bytes 4720241 | solution.py:71
  497.4 11.6 %pad_maximum_fusion.5 = bf16[2,96,96,192]{3,2,1,0:T(8,128)(2,1)} fusion(bf16[2,96,96,96]{3,2,1,0:T(8,128)(2,1)} %get-tuple-element.44), kind=kLoop, calls=%fused_computation.23 | loop fusion | flops 14155776 | bytes 10616832 | tf_op jit(solution)/shard_map/vmap(jit(_roll_dynamic))/concatenate | solution.py:72
  511.7 12.9 %while.11 = (s32[]{:T(128)}, bf16[2,96,96,192]{3,2,1,0:T(8,128)(2,1)}, s32[2,4]{1,0:T(2,128)S(1)}, bf16[2,96,96,96]{3,2,1,0:T(8,128)(2,1)}, s32[]{:T(128)}) while((s32[]{:T(128)}, bf16[2,96,96,192]{3,2,1,0:T(8,128)(2,1)}, s32[2,4]{1,0:T(2,128)S(1)}, bf16[2,96,96,96]{3,2,1,0:T(8,128)(2,1)}, s32[]{:T(128)}) %tuple.114), condition=%wide.while_cond.5, body=%wide.while_body.5.sunk | while | flops 2 | bytes 4720241 | solution.py:72
  535.5 105.1 %all-to-all-done.1 = bf16[12,24,96,32,2]{2,1,4,0,3:T(8,128)(2,1)} async-done(((bf16[12,24,96,32,2]{2,1,4,0,3:T(8,128)(2,1)}), bf16[12,24,96,32,2]{2,1,4,0,3:T(8,128)(2,1)}, u32[]{:S(2)}, u32[]{:S(2)}) %all-to-all-start.1) | async-done | bytes 3538976 | tf_op jit(solution)/shard_map/all_to_all | solution.py:80
  646.0 8.1 reshape_reshape.4
  654.1 12.0 %fusion.32 = f32[27648,256]{1,0:T(8,128)} fusion(bf16[27648,64]{0,1:T(8,128)(2,1)S(1)} %reshape_reshape.4, s32[64]{0:T(128)S(1)} %slice_bitcast_fusion), kind=kOutput, calls=%fused_computation.49 | convolution fusion | flops 905986048 | bytes 31850752 | tf_op jit(solution)/shard_map/dot_general | solution.py:83
  666.1 17.6 %fusion.28 = f32[256,256]{0,1:T(8,128)} fusion(bf16[27648,256]{1,0:T(8,128)(2,1)} %bitcast.109, f32[27648,256]{1,0:T(8,128)} %fusion.32), kind=kOutput, calls=%fused_computation.44 | convolution fusion | flops 3630956544 | bytes 42729472 | tf_op jit(solution)/shard_map/dot_general | solution.py:86
  683.8 31.6 %all-reduce.8.cloned.1.call-done = f32[256,256]{0,1:T(8,128)} async-done(((f32[256,256]{0,1:T(8,128)}), f32[256,256]{0,1:T(8,128)}) %all-reduce.8.cloned.1.call-update) | async-done | bytes 262160 | tf_op jit(solution)/shard_map/psum | solution.py:89
  715.5 74.4 %all-reduce.10.cloned.1.call-done = f32[256,256]{0,1:T(8,128)} async-done(((f32[256,256]{0,1:T(8,128)}), f32[256,256]{0,1:T(8,128)}) %all-reduce.10.cloned.1.call-update) | async-done | bytes 262160 | tf_op jit(solution)/shard_map/psum | solution.py:90
  789.8 25.2 %fusion = f32[27648,256]{1,0:T(8,128)} fusion(f32[27648,256]{1,0:T(8,128)} %fusion.32, bf16[27648,256]{1,0:T(8,128)(2,1)} %bitcast.110, f32[256,256]{0,1:T(8,128)} %all-reduce.10.cloned.1.call-done), kind=kOutput, calls=%fused_computation.15 | convolution fusion | flops 3631087616 | bytes 71041024 | tf_op jit(solution)/shard_map/dot_general | solution.py:92
  (82 shorter events, 120.3 us)
Async XLA Ops:
  71.9 7.9 copy-start
  71.9 8.9 %copy-start.2 = (s32[64]{0:T(128)S(1)}, s32[64]{0:T(128)}, u32[]{:S(2)}) copy-start(s32[64]{0:T(128)} %param.7) | copy-start | bytes 772
  71.9 216.8 %all-to-all-start = ((bf16[12,24,96,32,4]{2,1,4,0,3:T(8,128)(2,1)}), bf16[12,24,96,32,4]{2,1,4,0,3:T(8,128)(2,1)}, u32[]{:S(2)}, u32[]{:S(2)}) async-start(bf16[12,24,96,32,4]{2,1,4,0,3:T(8,128)(2,1)} %copy.46), calls=%async_computation | async-start | bytes 18874368 | tf_op jit(solution)/shard_map/all_to_all | solution.py:42
  528.3 7.2 copy-start.1
  531.9 108.8 %all-to-all-start.1 = ((bf16[12,24,96,32,2]{2,1,4,0,3:T(8,128)(2,1)}), bf16[12,24,96,32,2]{2,1,4,0,3:T(8,128)(2,1)}, u32[]{:S(2)}, u32[]{:S(2)}) async-start(bf16[12,24,96,32,2]{2,1,4,0,3:T(8,128)(2,1)} %copy.62), calls=%async_computation.1 | async-start | bytes 9437184 | tf_op jit(solution)/shard_map/all_to_all | solution.py:80
  535.5 180.0 %all-reduce.8.cloned.1.call-start = ((), (), s32[]{:S(2)}) async-start(), calls=%async_computation.2 | async-start | bytes 524288 | tf_op jit(solution)/shard_map/psum | solution.py:89
  683.8 106.1 %all-reduce.10.cloned.1.call-start = ((), (), s32[]{:S(2)}) async-start(), calls=%async_computation.3 | async-start | bytes 524288 | tf_op jit(solution)/shard_map/psum | solution.py:90
Sparse Core Ops, SparseCore 0:
  683.9 31.4 all-reduce.7
  718.8 71.0 all-reduce.9
